TPU v7x, 32 devices: a whole 2x2x4 slice. The times are simulated.
32 devices in a mesh: dp: 2 (over core), seq: 4 (over z), tensor: 4 (over y, x).
Axes of the slice: x: 2, y: 2, z: 4, core: 2. Of those that a mesh axis runs over, the one named last changes fastest.
Arguments:
- tokens: bfloat16 [256, 4, 5120], P('seq', 'dp'), parts along dimension 1, may hold values from -6 to 6
- w_query: bfloat16 [5120, 5120], P(None, 'tensor'), may hold values from -0.5 to 0.5, as said below
- w_key: bfloat16 [5120, 5120], P(None, 'tensor'), may hold values from -0.5 to 0.5, as said below
- w_value: bfloat16 [5120, 5120], P(None, 'tensor'), may hold values from -0.078125 to 0.078125
- w_out: bfloat16 [5120, 5120], P('tensor'), may hold values from -0.125 to 0.125
- gain_query: float32 [5120], P('tensor'), may hold values from 0.5 to 4
- gain_key: float32 [5120], P('tensor'), may hold values from 0.5 to 4
Outputs:
- attended: bfloat16 [256, 4, 5120], P(('seq', 'tensor'), 'dp'), parts along dimension 1
There are 2 independent parts, one for each index of `dp`. A program takes and returns all parts, laid end to end along the dimension named above; an argument that names none is the same for every part. Nothing has to cross between parts.
Inputs may be any that keep to these rules, and one draw needn't show every extreme that they name: `w_query`: entries of order 5120 ** -0.5 with unequal column scales. `w_key`: entries of order 5120 ** -0.5 with unequal column scales.
All inputs are finite; a program needn't handle non-finite values.
Results may differ from a plain program's by a relative error of at most 0.013.
The roundings to bfloat16 on the way count: a program that leaves them out, or rounds other values in their place, can miss the bound.
Values may be sent and summed in bfloat16 or wider, within the bound.
A program may use at most 256 MiB of HBM per device.

v0:
```python
import jax
import jax.numpy as jnp
from jax import lax
from jax.sharding import PartitionSpec as P

HEADS = 40
HEAD_DIM = 128


def rotary(field, positions):
    half = HEAD_DIM // 2
    shaped = field.reshape(field.shape[0], -1, HEAD_DIM)
    freqs = jnp.exp(-jnp.log(500000.0) * jnp.arange(half, dtype=jnp.float32) * 2.0 / HEAD_DIM)
    angle = positions.astype(jnp.float32)[:, None] * freqs[None, :]
    cosine = jnp.cos(angle)[:, None, :]
    sine = jnp.sin(angle)[:, None, :]
    first = shaped[..., :half]
    second = shaped[..., half:]
    turned = jnp.concatenate(
        [first * cosine - second * sine, second * cosine + first * sine], axis=-1
    )
    return turned.reshape(field.shape[0], -1)


def local(tokens, w_query, w_key, w_value, w_out, gain_query, gain_key):
    tok_rows = tokens.shape[0]
    seq_count = tokens.shape[1]
    local_width = w_query.shape[1]
    local_heads = local_width // HEAD_DIM
    width = HEADS * HEAD_DIM
    flat = tokens.reshape(tok_rows * seq_count, tokens.shape[2])
    query = jnp.dot(flat, w_query, preferred_element_type=jnp.float32)
    key_raw = jnp.dot(flat, w_key, preferred_element_type=jnp.float32)
    sum_query, sum_key = lax.psum(
        (jnp.sum(query * query, axis=1), jnp.sum(key_raw * key_raw, axis=1)), "tensor"
    )
    value = jnp.dot(flat, w_value, preferred_element_type=jnp.float32).astype(jnp.bfloat16)
    scale_q = lax.rsqrt(sum_query / width + 1e-06)
    scale_k = lax.rsqrt(sum_key / width + 1e-06)
    my_block = lax.axis_index("seq")
    positions = my_block * tok_rows + jnp.arange(tok_rows, dtype=jnp.int32)
    row_positions = (positions[:, None] + jnp.zeros((1, seq_count), jnp.int32)).reshape(-1)
    q_normed = rotary(query * scale_q[:, None] * gain_query[None, :], row_positions).astype(
        jnp.bfloat16
    )
    k_normed = rotary(key_raw * scale_k[:, None] * gain_key[None, :], row_positions).astype(
        jnp.bfloat16
    )
    q_heads = q_normed.reshape(tok_rows, seq_count, local_heads, HEAD_DIM)
    k_local = k_normed.reshape(tok_rows, seq_count, local_width)
    v_local = value.reshape(tok_rows, seq_count, local_width)
    factor = HEAD_DIM ** (-0.5)
    piece = (
        lax.all_gather(k_local, "seq", axis=0, tiled=True),
        lax.all_gather(v_local, "seq", axis=0, tiled=True),
    )
    key_pos = jnp.arange(piece[0].shape[0], dtype=jnp.int32)
    key_block = piece[0]
    count = key_block.shape[0]
    key_heads = key_block.reshape(count, seq_count, local_heads, HEAD_DIM)
    value_heads = piece[1].reshape(count, seq_count, local_heads, HEAD_DIM)
    scores = (
        jnp.einsum("qshd,kshd->shqk", q_heads, key_heads, preferred_element_type=jnp.float32)
        * factor
    )
    allowed = (key_pos[None, None, None, :] <= positions[None, None, :, None]) & (
        key_pos[None, None, None, :] >= 0
    )
    old_max = jnp.full((seq_count, local_heads, tok_rows), -1e30, jnp.float32)
    new_max = jnp.maximum(old_max, jnp.max(jnp.where(allowed, scores, -1e30), axis=3))
    expo = jnp.where(allowed, jnp.exp(scores - new_max[..., None]), 0.0)
    new_total = jnp.sum(expo, axis=3)
    added = jnp.einsum(
        "shqk,kshd->shqd",
        expo.astype(jnp.bfloat16),
        value_heads,
        preferred_element_type=jnp.float32,
    )
    final_state = (new_max, new_total, added)
    final_max, final_total, final_acc = final_state
    mixed = (final_acc / final_total[..., None]).astype(jnp.bfloat16)
    mixed = jnp.transpose(mixed, (2, 0, 1, 3)).reshape(tok_rows, seq_count, local_width)
    return lax.psum_scatter(
        jnp.dot(mixed, w_out, preferred_element_type=jnp.float32).astype(jnp.bfloat16),
        "tensor",
        scatter_dimension=0,
        tiled=True,
    )


def solution(mesh):
    return jax.shard_map(
        local,
        mesh=mesh,
        in_specs=(
            P("seq", "dp", None),
            P(None, "tensor"),
            P(None, "tensor"),
            P(None, "tensor"),
            P("tensor", None),
            P("tensor"),
            P("tensor"),
        ),
        out_specs=P(("seq", "tensor"), "dp", None),
        check_vma=False,
    )
```

profile of v0, /device:TPU:24, one launch (start us, length us, event | category | flops | bytes accessed | tf_op | source)
XLA Modules:
  0.0 147.2 jit_solution(5699361693180010124)
XLA Ops:
  6.8 3.1 %reshape.132 = bf16[128,5120]{1,0:T(8,128)(2,1)S(1)} reshape(bf16[64,2,5120]{2,1,0:T(2,128)(2,1)} %param.7) | data formatting | bytes 2621440 | tf_op jit(solution)/shard_map/reshape | solution.py:31
  9.9 6.8 %multiply_reduce_fusion.1 = (f32[128]{0:T(128)S(1)}, f32[128,1280]{1,0:T(8,128)S(1)}) fusion(bf16[128,5120]{1,0:T(8,128)(2,1)S(1)} %reshape.132, bf16[5120,1280]{1,0:T(8,128)(2,1)} %param.8), kind=kOutput, calls=%fused_computation.18 | convolution fusion | flops 1678049152 | bytes 15073792 | tf_op jit(solution)/shard_map/dot_general | solution.py:32
  16.7 1.6 %copy-done = bf16[5120,1280]{1,0:T(8,128)(2,1)S(1)} copy-done((bf16[5120,1280]{1,0:T(8,128)(2,1)S(1)}, bf16[5120,1280]{1,0:T(8,128)(2,1)}, u32[]{:S(2)}) %copy-start) | copy-done | bytes 13107224
  18.4 2.0 %multiply_reduce_fusion = (f32[128]{0:T(128)S(1)}, f32[128,1280]{1,0:T(8,128)S(1)}) fusion(bf16[128,5120]{1,0:T(8,128)(2,1)S(1)} %reshape.132, bf16[5120,1280]{1,0:T(8,128)(2,1)S(1)} %copy-done), kind=kOutput, calls=%fused_computation.16 | convolution fusion | flops 1678049152 | bytes 15073792 | tf_op jit(solution)/shard_map/dot_general | solution.py:33
  20.3 9.9 %all-reduce = (f32[128]{0:T(128)S(1)}, f32[128]{0:T(128)S(1)}) all-reduce(f32[128]{0:T(128)S(1)} %get-tuple-element.15, f32[128]{0:T(128)S(1)} %get-tuple-element.17), channel_id=1, replica_groups=mesh['dp'=2,'seq'=4,'tensor'=4] {'tensor'}, use_global_device_ids=true, to_apply=%region_3.0 | all-reduce | flops 256 | bytes 2048 | tf_op jit(solution)/shard_map/psum | solution.py:34
  30.4 0.2 copy.22
  30.6 0.3 copy-done.2
  31.1 0.2 copy.20
  31.7 0.4 copy.23
  32.2 0.9 convert_element_type.38
  33.1 6.6 %convolution_convert_fusion = bf16[128,1280]{1,0:T(8,128)(2,1)S(1)} fusion(bf16[128,5120]{1,0:T(8,128)(2,1)S(1)} %reshape.132, bf16[5120,1280]{1,0:T(8,128)(2,1)} %param.10), kind=kOutput, calls=%fused_computation.3 | convolution fusion | flops 1677885440 | bytes 14745600 | tf_op jit(solution)/shard_map/dot_general | solution.py:37
  39.8 0.8 reshape.136
  40.6 0.2 reduce-scatter.2.cloned.1.call-start
  40.9 0.2 copy.21
  41.2 21.8 %all-gather.3.cloned.1.call-done = bf16[256,2,1280]{2,1,0:T(2,128)(2,1)} async-done(((bf16[64,2,1280]{2,1,0:T(2,128)(2,1)}), bf16[256,2,1280]{2,1,0:T(2,128)(2,1)}) %all-gather.3.cloned.1.call-update) | async-done | bytes 1310736 | tf_op jit(solution)/shard_map/all_gather | solution.py:54
  63.1 3.3 %copy.24 = bf16[256,2,1280]{0,2,1:T(8,128)(2,1)S(1)} copy(bf16[256,2,1280]{2,1,0:T(2,128)(2,1)} %all-gather.3.cloned.1.call-done) | data formatting | bytes 2621440 | tf_op jit(solution)/shard_map/all_gather | solution.py:54
  66.4 0.4 select_reduce_fusion
  66.9 0.5 fusion.8
  67.4 28.9 %all-gather.5.cloned.1.call-done = bf16[256,2,1280]{2,1,0:T(2,128)(2,1)} async-done(((bf16[64,2,1280]{2,1,0:T(2,128)(2,1)}), bf16[256,2,1280]{2,1,0:T(2,128)(2,1)}) %all-gather.5.cloned.1.call-update) | async-done | bytes 1310736 | tf_op jit(solution)/shard_map/all_gather | solution.py:55
  96.3 3.3 %copy.27 = bf16[256,2,1280]{0,2,1:T(8,128)(2,1)S(1)} copy(bf16[256,2,1280]{2,1,0:T(2,128)(2,1)} %all-gather.5.cloned.1.call-done) | data formatting | bytes 2621440 | tf_op jit(solution)/shard_map/all_gather | solution.py:55
  99.6 0.6 fusion.7
  100.3 7.8 %fusion.2 = bf16[64,2,5120]{2,0,1:T(8,128)(2,1)} fusion(bf16[1280,5120]{1,0:T(8,128)(2,1)} %param.11, bf16[2,10,8,8,128]{4,3,2,1,0:T(8,128)(2,1)S(1)} %fusion.7), kind=kOutput, calls=%fused_computation.2 | convolution fusion | flops 1678376960 | bytes 14745600 | tf_op jit(solution)/shard_map/dot_general | solution.py:84
  108.1 30.6 %reduce-scatter.2.cloned.1.call-done = bf16[16,2,5120]{2,0,1:T(8,128)(2,1)} async-done(((bf16[64,2,5120]{2,0,1:T(8,128)(2,1)}), bf16[16,2,5120]{2,0,1:T(8,128)(2,1)}) %reduce-scatter.2.cloned.1.call-update) | async-done | bytes 327696 | tf_op jit(solution)/shard_map/reduce_scatter | solution.py:83
  138.7 2.0 %copy.30 = bf16[16,2,5120]{2,1,0:T(2,128)(2,1)} copy(bf16[16,2,5120]{2,0,1:T(8,128)(2,1)} %reduce-scatter.2.cloned.1.call-done) | data formatting | bytes 655360 | tf_op jit(solution)/shard_map/reduce_scatter | solution.py:83
  (23 shorter events, 1.1 us)
Async XLA Ops:
  6.5 56.5 %all-gather.3.cloned.1.call-start = ((), (), s32[]{:S(2)}) async-start(), calls=%async_computation.1 | async-start | bytes 1638400 | tf_op jit(solution)/shard_map/all_gather | solution.py:54
  9.9 8.5 %copy-start = (bf16[5120,1280]{1,0:T(8,128)(2,1)S(1)}, bf16[5120,1280]{1,0:T(8,128)(2,1)}, u32[]{:S(2)}) copy-start(bf16[5120,1280]{1,0:T(8,128)(2,1)} %param.9) | copy-start | bytes 39321604
  18.4 11.9 %copy-start.1 = (f32[1280]{0:T(1024)S(1)}, f32[1280]{0:T(1024)}, u32[]{:S(2)}) copy-start(f32[1280]{0:T(1024)} %param.13) | copy-start | bytes 15364
  30.2 0.7 copy-start.2
  33.1 63.2 %all-gather.5.cloned.1.call-start = ((), (), s32[]{:S(2)}) async-start(), calls=%async_computation.2 | async-start | bytes 1638400 | tf_op jit(solution)/shard_map/all_gather | solution.py:55
  40.6 98.0 %reduce-scatter.2.cloned.1.call-start = ((), (), s32[]{:S(2)}) async-start(), calls=%async_computation.3 | async-start | bytes 1638400 | tf_op jit(solution)/shard_map/reduce_scatter | solution.py:83
Sparse Core Ops, SparseCore 0:
  33.2 29.7 all-gather.2
  64.6 31.6 all-gather.4
  108.2 30.4 reduce-scatter.1
where the time goes:
time: 149 us; the launch traced here: 147 us
  waiting for transfers between devices  81.4 us (55%)
  matrix products  24.3 us (16%)
  local copies, waits for them, and re-layouts  16.8 us (11%)
  between operations  13.3 us (9%)
  blocking collectives  9.92 us (7%)
    reduce_scatter x1, waiting for transfers between devices, local(): lax.psum_scatter(jnp.dot(mixed, w_out, preferred_element_type=jnp.float32...  30.6 us
    all_gather x1, waiting for transfers between devices, local(): lax.all_gather(v_local, 'seq', axis=0, tiled=True)  28.9 us
    all_gather x1, waiting for transfers between devices, local(): lax.all_gather(k_local, 'seq', axis=0, tiled=True)  21.8 us
    psum x1, blocking collectives, local(): lax.psum((jnp.sum(query * query, axis=1), jnp.sum(key_raw * key_raw, axis...  9.92 us
    dot_general x1, matrix products, local(): jnp.dot(mixed, w_out, preferred_element_type=jnp.float32)  7.82 us
    dot_general x1, matrix products, local(): query = jnp.dot(flat, w_query, preferred_element_type=jnp.float32)  6.83 us
    dot_general x1, matrix products, local(): jnp.dot(flat, w_value, preferred_element_type=jnp.float32)  6.6 us
    all_gather x1, local copies, waits for them, and re-layouts, local(): lax.all_gather(k_local, 'seq', axis=0, tiled=True)  3.34 us
  transfers between devices with their start and end apart: 3, of which 3 were waited for; matrix products, arithmetic and copies ran while one was open for 8% of the time, Pallas kernels for 0%

commit v1 on v0

--- a/solution.py
+++ b/solution.py
@@ -1,10 +1,393 @@
+import functools
+
 import jax
 import jax.numpy as jnp
 from jax import lax
+from jax.experimental import pallas as pl
+from jax.experimental.pallas import tpu as pltpu
 from jax.sharding import PartitionSpec as P
 
 HEADS = 40
 HEAD_DIM = 128
+MESH = pl.DeviceIdType.MESH
+COLS = 2 * HEAD_DIM
+RING = 5
+F32 = jnp.float32
+BF16 = jnp.bfloat16
+
+
+def block_kernel(
+    ns, nt, tok, width,
+    x_ref, cos_ref, sin_ref, gq_ref, gk_ref, wq, wk, wv, wo,
+    out_ref,
+    ring, wov, sq, sk, sums_out, sums_in, rqs, rks,
+    qbuf, kbuf, vbuf, own_o, own_lse, oout, lse_out, oin, lse_in,
+    mixed, part, rs_in,
+    w_sem, wo_sem, sum_send, sum_recv, k_send, k_recv, v_send, v_recv,
+    q_send, q_recv, o_send, o_recv, l_send, l_recv, rs_send, rs_recv,
+):
+    dp = lax.axis_index("dp")
+    z = lax.axis_index("seq")
+    me = lax.axis_index("tensor")
+    nc = qbuf.shape[0]
+    rows = 2 * tok
+    oc = wov.shape[2]
+    no = wov.shape[0]
+
+    def w_copy(kind, c, slot):
+        ref = (wk, wq, wv)[kind]
+        return pltpu.make_async_copy(
+            ref.at[:, pl.ds(pl.multiple_of(c * COLS, COLS), COLS)], ring.at[slot], w_sem.at[slot]
+        )
+
+    def wo_copy(c):
+        return pltpu.make_async_copy(
+            wo.at[:, pl.ds(pl.multiple_of(c * oc, oc), oc)], wov.at[c], wo_sem.at[c]
+        )
+
+    def start(i):
+        slot = lax.rem(i, RING)
+
+        @pl.when((i < 2 * nc) & (lax.rem(i, 2) == 0))
+        def _():
+            w_copy(0, i // 2, slot).start()
+
+        @pl.when((i < 2 * nc) & (lax.rem(i, 2) == 1))
+        def _():
+            w_copy(1, i // 2, slot).start()
+
+        @pl.when((i >= 2 * nc) & (i < 3 * nc))
+        def _():
+            w_copy(2, i - 2 * nc, slot).start()
+
+        @pl.when((i >= 3 * nc) & (i < 3 * nc + no))
+        def _():
+            wo_copy(i - 3 * nc).start()
+
+    for i in range(RING - 1):
+        w_copy(i % 2, i // 2, i).start()
+
+    barrier = pltpu.get_barrier_semaphore()
+    peers = []
+    for dz in range(ns):
+        for dk in range(nt):
+            if dz or dk:
+                peers.append((dp, lax.rem(z + dz, ns), lax.rem(me + dk, nt)))
+    for peer in peers:
+        pl.semaphore_signal(barrier, inc=1, device_id=peer, device_id_type=MESH)
+    pl.semaphore_wait(barrier, len(peers))
+
+    def remote(src, dst, ssem, rsem, to):
+        return pltpu.make_async_remote_copy(
+            src_ref=src, dst_ref=dst, send_sem=ssem, recv_sem=rsem, device_id=to, device_id_type=MESH
+        )
+
+    def k_copy(c, to):
+        return remote(kbuf.at[c, :, pl.ds(0, tok)], kbuf.at[c, :, pl.ds(tok, tok)], k_send.at[c], k_recv.at[c], (dp, to, me))
+
+    def v_copy(c, to):
+        return remote(vbuf.at[c, :, pl.ds(0, tok)], vbuf.at[c, :, pl.ds(tok, tok)], v_send.at[c], v_recv.at[c], (dp, to, me))
+
+    def q_copy(c, s, to):
+        return remote(qbuf.at[c, :, pl.ds(0, tok)], qbuf.at[c, :, pl.ds(s * tok, tok)], q_send.at[s - 1, c], q_recv.at[s - 1, c], (dp, to, me))
+
+    def o_copy(c, s, to):
+        return remote(oout.at[s - 1, c], oin.at[s - 1, c], o_send.at[s - 1, c], o_recv.at[s - 1, c], (dp, to, me))
+
+    def l_copy(s, to):
+        return remote(lse_out.at[s - 1], lse_in.at[s - 1], l_send.at[s - 1], l_recv.at[s - 1], (dp, to, me))
+
+    def product(kind, i):
+        slot = lax.rem(i, RING)
+        start(i + RING - 1)
+        w_copy(kind, 0, slot).wait()
+        return jnp.dot(x_ref[...], ring[slot], preferred_element_type=F32)
+
+    def turned(acc, gain, c, buf):
+        cosine, sine = cos_ref[...], sin_ref[...]
+        for h in range(2):
+            y = acc[:, h * HEAD_DIM : (h + 1) * HEAD_DIM] * gain[c, :, h * HEAD_DIM : (h + 1) * HEAD_DIM]
+            y = (y * cosine + pltpu.roll(y, HEAD_DIM // 2, 1) * sine).astype(BF16)
+            for j in range(2):
+                buf[c, j, 0:tok, h * HEAD_DIM : (h + 1) * HEAD_DIM] = y[j * tok : (j + 1) * tok]
+
+    sq[...] = jnp.zeros_like(sq)
+    sk[...] = jnp.zeros_like(sk)
+
+    @pl.loop(0, nc)
+    def _(c):
+        acc = product(0, 2 * c)
+        sk[...] += acc[:, :HEAD_DIM] * acc[:, :HEAD_DIM] + acc[:, HEAD_DIM:] * acc[:, HEAD_DIM:]
+        turned(acc, gk_ref, c, kbuf)
+
+        @pl.when(z == 0)
+        def _():
+            k_copy(c, 1).start()
+
+        acc = product(1, 2 * c + 1)
+        sq[...] += acc[:, :HEAD_DIM] * acc[:, :HEAD_DIM] + acc[:, HEAD_DIM:] * acc[:, HEAD_DIM:]
+        turned(acc, gq_ref, c, qbuf)
+
+        @pl.when(z == 3)
+        def _():
+            q_copy(c, 2, 1).start()
+            q_copy(c, 1, 2).start()
+
+        @pl.when(z == 2)
+        def _():
+            q_copy(c, 1, 1).start()
+
+    sums_out[...] = jnp.zeros_like(sums_out)
+    sums_out[0:1, :] = jnp.sum(jnp.transpose(sq[...]), axis=0, keepdims=True)
+    sums_out[1:2, :] = jnp.sum(jnp.transpose(sk[...]), axis=0, keepdims=True)
+    mine = z * nt + me
+    sends = []
+    for n, peer in enumerate(peers):
+        copy = remote(sums_out, sums_in.at[n], sum_send.at[n], sum_recv.at[n], peer)
+        copy.start()
+        sends.append(copy)
+
+    @pl.loop(0, nc)
+    def _(c):
+        acc = product(2, 2 * nc + c).astype(BF16)
+        for j in range(2):
+            vbuf[c, j, 0:tok, :] = acc[j * tok : (j + 1) * tok]
+
+        @pl.when(z == 0)
+        def _():
+            v_copy(c, 1).start()
+
+    for c in range(max(0, RING - 1), no):
+        wo_copy(c).start()
+
+    for copy in sends:
+        copy.wait()
+
+    def total(back):
+        tot = sums_out[...] if back == 0 else None
+        n = 0
+        for dz in range(ns):
+            for dk in range(nt):
+                if dz or dk:
+                    if dz == back:
+                        tot = sums_in[n] if tot is None else tot + sums_in[n]
+                    n += 1
+        return lax.rsqrt(tot / width + 1e-06)
+
+    r0 = total(0)
+    ahead = [r0, total(ns - 1), total(ns - 2)]
+    factor = HEAD_DIM ** (-0.5)
+    for s in range(3):
+        rqs[s] = jnp.transpose(jnp.broadcast_to(ahead[s][0:1, :] * factor, (rows, rows)))
+    r1 = total(1)
+    low = lax.broadcasted_iota(jnp.int32, r0.shape, 1) < tok
+    rks[0] = jnp.where(low, r0, pltpu.roll(r1, tok, 1))
+    rks[1] = jnp.where(low, pltpu.roll(r0, tok, 1), r1)
+
+    def attend(nq, nk, has_in):
+        own_lse[...] = jnp.zeros_like(own_lse)
+        if nq > 1:
+            lse_out[...] = jnp.zeros_like(lse_out)
+        lane = lax.broadcasted_iota(jnp.int32, (tok, HEAD_DIM), 1)
+        row = lax.broadcasted_iota(jnp.int32, (tok, nk * tok), 0)
+        col = lax.broadcasted_iota(jnp.int32, (tok, nk * tok), 1)
+        allowed = (col <= row) | (col >= tok)
+
+        @pl.loop(0, nc)
+        def _(c):
+            for s in range(1, nq):
+                q_copy(c, s, z).wait_recv()
+            if nk > 1:
+                k_copy(c, z).wait_recv()
+                v_copy(c, z).wait_recv()
+            for j in range(2):
+                for h in range(2):
+                    hs = slice(h * HEAD_DIM, (h + 1) * HEAD_DIM)
+                    u = c * 4 + j * 2 + h
+                    k = kbuf[c, j, 0 : nk * tok, hs]
+                    v = vbuf[c, j, 0 : nk * tok, hs]
+                    q = qbuf[c, j, 0 : nq * tok, hs]
+                    score = lax.dot_general(q, k, (((1,), (1,)), ((), ())), preferred_element_type=F32)
+                    weights, tots, tops = [], [], []
+                    for s in range(nq):
+                        sc = score[s * tok : (s + 1) * tok]
+                        sc = sc * rqs[s, j * tok : (j + 1) * tok, 0 : nk * tok] * rks[j, 1:2, 0 : nk * tok]
+                        if s == 0:
+                            sc = jnp.where(allowed, sc, -1e30)
+                        top = jnp.max(sc, axis=1, keepdims=True)
+                        e = jnp.exp(sc - top)
+                        tots.append(jnp.sum(e, axis=1, keepdims=True))
+                        tops.append(top)
+                        weights.append(e.astype(BF16))
+                    w = weights[0] if nq == 1 else jnp.concatenate(weights, axis=0)
+                    acc = jnp.dot(w, v, preferred_element_type=F32)
+                    for s in range(nq):
+                        o = acc[s * tok : (s + 1) * tok] / tots[s]
+                        if s == 0 and not has_in:
+                            mixed[j * tok : (j + 1) * tok, pl.ds(pl.multiple_of(c * COLS + h * HEAD_DIM, HEAD_DIM), HEAD_DIM)] = o.astype(BF16)
+                        elif s == 0:
+                            own_o[c, j, :, hs] = o
+                            own_lse[...] = jnp.where(lane == u, tops[s] + jnp.log(tots[s]), own_lse[...])
+                        else:
+                            oout[s - 1, c, j, :, hs] = o.astype(BF16)
+                            lse_out[s - 1] = jnp.where(lane == u, tops[s] + jnp.log(tots[s]), lse_out[s - 1])
+            for s in range(1, nq):
+                o_copy(c, s, z + s).start()
+
+        for s in range(1, nq):
+            l_copy(s, z + s).start()
+
+    def merge(ni):
+        lane = lax.broadcasted_iota(jnp.int32, (tok, HEAD_DIM), 1)
+        for s in range(1, ni + 1):
+            l_copy(s, z).wait_recv()
+        lses = [own_lse[...]] + [lse_in[s] for s in range(ni)]
+        top = functools.reduce(jnp.maximum, lses)
+        parts = [jnp.exp(v - top) for v in lses]
+        tot = functools.reduce(jnp.add, parts)
+        for s in range(ni + 1):
+            rqs[s, 0:tok] = parts[s] / tot
+
+        @pl.loop(0, nc)
+        def _(c):
+            for s in range(1, ni + 1):
+                o_copy(c, s, z).wait_recv()
+            for j in range(2):
+                for h in range(2):
+                    hs = slice(h * HEAD_DIM, (h + 1) * HEAD_DIM)
+                    u = c * 4 + j * 2 + h
+                    o = 0.0
+                    for s in range(ni + 1):
+                        share = jnp.sum(jnp.where(lane == u, rqs[s, 0:tok], 0.0), axis=1, keepdims=True)
+                        o += share * (own_o[c, j, :, hs] if s == 0 else oin[s - 1, c, j, :, hs].astype(F32))
+                    mixed[j * tok : (j + 1) * tok, pl.ds(pl.multiple_of(c * COLS + h * HEAD_DIM, HEAD_DIM), HEAD_DIM)] = o.astype(BF16)
+
+    @pl.when(z == 0)
+    def _():
+        attend(1, 1, False)
+
+    @pl.when(z == 1)
+    def _():
+        attend(3, 2, False)
+
+    @pl.when(z == 2)
+    def _():
+        attend(2, 1, True)
+        merge(1)
+
+    @pl.when(z == 3)
+    def _():
+        attend(1, 1, True)
+        merge(2)
+
+    share = tok // nt
+
+    def rs_copy(c, d):
+        to = lax.rem(me + d, nt)
+        return remote(
+            part.at[c, :, pl.ds(pl.multiple_of(to * share, share), share)], rs_in.at[d - 1, c],
+            rs_send.at[d - 1, c], rs_recv.at[d - 1, c], (dp, z, to),
+        )
+
+    @pl.loop(0, no)
+    def _(c):
+        wo_copy(c).wait()
+        acc = jnp.dot(mixed[...], wov[c], preferred_element_type=F32).astype(BF16)
+        for j in range(2):
+            part[c, j] = acc[j * tok : (j + 1) * tok]
+        for d in range(1, nt):
+            rs_copy(c, d).start()
+
+    @pl.loop(0, no)
+    def _(c):
+        for d in range(1, nt):
+            rs_copy(c, d).wait_recv()
+        for j in range(2):
+            o = part[c, j, pl.ds(pl.multiple_of(me * share, share), share)].astype(F32)
+            for d in range(1, nt):
+                o += rs_in[d - 1, c, j].astype(F32)
+            out_ref[j, :, pl.ds(pl.multiple_of(c * oc, oc), oc)] = o.astype(BF16)
+        for d in range(1, nt):
+            rs_copy(c, d).wait_send()
+
+    @pl.loop(0, nc)
+    def _(c):
+        @pl.when(z == 0)
+        def _():
+            k_copy(c, 1).wait_send()
+            v_copy(c, 1).wait_send()
+
+        @pl.when(z == 3)
+        def _():
+            q_copy(c, 2, 1).wait_send()
+            q_copy(c, 1, 2).wait_send()
+
+        @pl.when(z == 2)
+        def _():
+            q_copy(c, 1, 1).wait_send()
+            o_copy(c, 1, 3).wait_send()
+
+        @pl.when(z == 1)
+        def _():
+            o_copy(c, 1, 2).wait_send()
+            o_copy(c, 2, 3).wait_send()
+
+    @pl.when(z == 2)
+    def _():
+        l_copy(1, 3).wait_send()
+
+    @pl.when(z == 1)
+    def _():
+        l_copy(1, 2).wait_send()
+        l_copy(2, 3).wait_send()
+
+
+def fused(ns, nt, tokens, w_query, w_key, w_value, w_out, gain_query, gain_key):
+    tok, seqs, depth = tokens.shape
+    local = w_query.shape[1]
+    nc = local // COLS
+    oc = 1024
+    no = depth // oc
+    rows = tok * seqs
+    width = HEADS * HEAD_DIM
+    x = jnp.transpose(tokens, (1, 0, 2)).reshape(rows, depth)
+    half = HEAD_DIM // 2
+    freqs = jnp.exp(-jnp.log(500000.0) * jnp.arange(half, dtype=F32) * 2.0 / HEAD_DIM)
+    positions = lax.axis_index("seq") * tok + jnp.arange(rows, dtype=jnp.int32) % tok
+    angle = positions.astype(F32)[:, None] * freqs[None, :]
+    cosine, sine = jnp.cos(angle), jnp.sin(angle)
+    cosine = jnp.concatenate([cosine, cosine], axis=1)
+    sine = jnp.concatenate([-sine, sine], axis=1)
+    peers = ns * nt - 1
+    vm = pltpu.VMEM
+    dma = pltpu.SemaphoreType.DMA
+    tile = (tok, HEAD_DIM)
+    scratch = [
+        vm((RING, depth, COLS), BF16), vm((no, local, oc), BF16),
+        vm((rows, HEAD_DIM), F32), vm((rows, HEAD_DIM), F32),
+        vm((8, rows), F32), vm((peers, 8, rows), F32),
+        vm((3, rows, rows), F32), vm((2, 8, rows), F32),
+        vm((nc, seqs, 3 * tok, COLS), BF16), vm((nc, seqs, 2 * tok, COLS), BF16), vm((nc, seqs, 2 * tok, COLS), BF16),
+        vm((nc, seqs, tok, COLS), F32), vm(tile, F32),
+        vm((2, nc, seqs, tok, COLS), BF16), vm((2,) + tile, F32),
+        vm((2, nc, seqs, tok, COLS), BF16), vm((2,) + tile, F32),
+        vm((rows, local), BF16), vm((no, seqs, tok, oc), BF16), vm((nt - 1, no, seqs, tok // nt, oc), BF16),
+        dma((RING,)), dma((no,)), dma((peers,)), dma((peers,)),
+        dma((nc,)), dma((nc,)), dma((nc,)), dma((nc,)),
+        dma((2, nc)), dma((2, nc)), dma((2, nc)), dma((2, nc)), dma((2,)), dma((2,)),
+        dma((nt - 1, no)), dma((nt - 1, no)),
+    ]
+    in_vmem = pl.BlockSpec(memory_space=pltpu.VMEM)
+    anywhere = pl.BlockSpec(memory_space=pl.ANY)
+    out = pl.pallas_call(
+        functools.partial(block_kernel, ns, nt, tok, width),
+        out_shape=jax.ShapeDtypeStruct((seqs, tok // nt, depth), BF16),
+        in_specs=[in_vmem] * 5 + [anywhere] * 4,
+        out_specs=in_vmem,
+        scratch_shapes=scratch,
+        compiler_params=pltpu.CompilerParams(collective_id=0, has_side_effects=True, vmem_limit_bytes=60 * 1024 * 1024),
+    )(x, cosine, sine, gain_query.reshape(nc, 1, COLS), gain_key.reshape(nc, 1, COLS), w_query, w_key, w_value, w_out)
+    return jnp.transpose(out, (1, 0, 2))
 
 
 def rotary(field, positions):
@@ -89,8 +472,10 @@
 
 
 def solution(mesh):
+    ns, nt = mesh.shape["seq"], mesh.shape["tensor"]
+    step = functools.partial(fused, ns, nt) if ns == 4 and nt == 4 else local
     return jax.shard_map(
-        local,
+        step,
         mesh=mesh,
         in_specs=(
             P("seq", "dp", None),

time: 149 us -> 68.7 us (0.46); the launches traced: 147 us -> 68.4 us
  waiting for transfers between devices: 81.4 us -> 0 us
  Pallas kernels: 0 us -> 60.1 us
  matrix products: 24.3 us -> 0 us
  between operations: 13.3 us -> 0.02 us
  blocking collectives: 9.92 us -> 0 us
  local copies, waits for them, and re-layouts: 16.8 us -> 7.27 us
    pallas_call x0 -> x1, Pallas kernels: none -> 60.1 us  [fused(): pl.pallas_call(functools.partial(block_kernel, ns, nt, tok, width), out_s...]
    all_gather x2 -> x0, waiting for transfers between devices: 50.8 us -> none  [the longest x1 28.9 us: local(): lax.all_gather(v_local, 'seq', axis=0, tiled=True)]
    reduce_scatter x1 -> x0, waiting for transfers between devices: 30.6 us -> none  [local(): lax.psum_scatter(jnp.dot(mixed, w_out, preferred_element_type=jnp.float32...]
    dot_general x6 -> x0, matrix products: 24.3 us -> none  [the longest x1 7.82 us: local(): jnp.dot(mixed, w_out, preferred_element_type=jnp.float32)]
    psum x1 -> x0, blocking collectives: 9.92 us -> none  [local(): lax.psum((jnp.sum(query * query, axis=1), jnp.sum(key_raw * key_raw, axis...]
    all_gather x2 -> x0, local copies, waits for them, and re-layouts: 6.68 us -> none  [the longest x1 3.34 us: local(): lax.all_gather(k_local, 'seq', axis=0, tiled=True)]
    transpose x0 -> x2, local copies, waits for them, and re-layouts: none -> 4.67 us  [the longest x1 2.64 us: fused(): x = jnp.transpose(tokens, (1, 0, 2)).reshape(rows, depth)]
    reduce_scatter x1 -> x0, local copies, waits for them, and re-layouts: 2.03 us -> none  [local(): lax.psum_scatter(jnp.dot(mixed, w_out, preferred_element_type=jnp.float32...]
  transfers between devices with their start and end apart: 3 -> 0, of which waited for: 3 -> 0; matrix products, arithmetic and copies ran while one was open for 8% -> 0% of each run, Pallas kernels for 0% -> 0%
where the time goes in v1:
time: 68.7 us; the launch traced here: 68.4 us
  Pallas kernels  60.1 us (87%)
  local copies, waits for them, and re-layouts  7.27 us (11%)
  other arithmetic  1.07 us (2%)
    pallas_call x1, Pallas kernels, fused(): pl.pallas_call(functools.partial(block_kernel, ns, nt, tok, width), out_s...  60.1 us
    transpose x1, local copies, waits for them, and re-layouts, fused(): x = jnp.transpose(tokens, (1, 0, 2)).reshape(rows, depth)  2.64 us
    transpose x1, local copies, waits for them, and re-layouts, fused(): return jnp.transpose(out, (1, 0, 2))  2.03 us

profile of v1, /device:TPU:24, one launch (start us, length us, event | category | flops | bytes accessed | tf_op | source)
XLA Modules:
  0.0 68.4 jit_solution(9975009877279104571)
XLA Ops:
  0.0 1.3 %reshape.26.gq_ref = f32[5,1,256]{2,1,0:T(1,128)} reshape(f32[1280]{0:T(1024)} %param.12) | data formatting | bytes 10240 | tf_op jit(solution)/shard_map/reshape | solution.py:389
  1.3 1.3 %reshape.27.gk_ref = f32[5,1,256]{2,1,0:T(1,128)} reshape(f32[1280]{0:T(1024)} %param.13) | data formatting | bytes 10240 | tf_op jit(solution)/shard_map/reshape | solution.py:389
  2.6 0.3 fusion
  2.9 0.7 %pad_maximum_fusion = (f32[128,128]{1,0:T(8,128)}, f32[128,128]{1,0:T(8,128)}) fusion(f32[128,64]{1,0:T(8,128)S(1)} %get-tuple-element.7, f32[128,64]{1,0:T(8,128)S(1)} %get-tuple-element.6, f32[128,64]{1,0:T(8,128)S(1)} %get-tuple-element.5), kind=kLoop, calls=%fused_computation.2 | loop fusion | flops 32768 | bytes 229376 | tf_op jit(solution)/shard_map/concatenate | solution.py:359
  3.7 2.6 %copy.8 = bf16[2,64,5120]{2,1,0:T(8,128)(2,1)} copy(bf16[2,64,5120]{2,0,1:T(2,128)(2,1)} %bitcast.5) | data formatting | bytes 2621440 | tf_op jit(solution)/shard_map/transpose | solution.py:353
  6.3 60.1 %shard_map.73 = bf16[2,16,5120]{2,1,0:T(8,128)(2,1)} custom-call(bf16[128,5120]{1,0:T(8,128)(2,1)} %bitcast.3, f32[128,128]{1,0:T(8,128)} %get-tuple-element.8.cos_ref, f32[128,128]{1,0:T(8,128)} %get-tuple-element.9.sin_ref, f32[5,1,256]{2,1,0:T(1,128)} %reshape.26.gq_ref, f32[5,1,256]{2,1,0:T(1,128)} %reshape.27.gk_ref, bf16[5120,1280]{1,0:T(8,128)(2,1)} %wq.1, ...), custom_call_target="tpu_custom_call" | custom-call | tf_op jit(solution)/shard_map/pallas_call | solution.py:382
  66.4 2.0 %copy.9 = bf16[16,2,5120]{2,1,0:T(2,128)(2,1)} copy(bf16[16,2,5120]{2,0,1:T(8,128)(2,1)} %bitcast.4) | data formatting | bytes 655360 | tf_op jit(solution)/shard_map/transpose | solution.py:390
  (2 shorter events, 0.0 us)

commit v2 on v1

--- a/solution.py
+++ b/solution.py
@@ -11,16 +11,16 @@
 HEAD_DIM = 128
 MESH = pl.DeviceIdType.MESH
 COLS = 2 * HEAD_DIM
-RING = 5
+RING = 9
 F32 = jnp.float32
 BF16 = jnp.bfloat16
 
 
 def block_kernel(
     ns, nt, tok, width,
-    x_ref, cos_ref, sin_ref, gq_ref, gk_ref, wq, wk, wv, wo,
+    x_ref, gq_in, gk_in, wq, wk, wv, wo,
     out_ref,
-    ring, wov, sq, sk, sums_out, sums_in, rqs, rks,
+    ring, wov, cos_ref, sin_ref, gq_ref, gk_ref, sq, sk, sums_out, sums_in, rqs, rks,
     qbuf, kbuf, vbuf, own_o, own_lse, oout, lse_out, oin, lse_in,
     mixed, part, rs_in,
     w_sem, wo_sem, sum_send, sum_recv, k_send, k_recv, v_send, v_recv,
@@ -75,7 +75,6 @@
                 peers.append((dp, lax.rem(z + dz, ns), lax.rem(me + dk, nt)))
     for peer in peers:
         pl.semaphore_signal(barrier, inc=1, device_id=peer, device_id_type=MESH)
-    pl.semaphore_wait(barrier, len(peers))
 
     def remote(src, dst, ssem, rsem, to):
         return pltpu.make_async_remote_copy(
@@ -111,12 +110,31 @@
             for j in range(2):
                 buf[c, j, 0:tok, h * HEAD_DIM : (h + 1) * HEAD_DIM] = y[j * tok : (j + 1) * tok]
 
+    lanes = lax.broadcasted_iota(jnp.int32, (tok, HEAD_DIM), 1)
+    half = HEAD_DIM // 2
+    freqs = jnp.exp(-jnp.log(500000.0) * lax.rem(lanes, half).astype(F32) * 2.0 / HEAD_DIM)
+    spot = z * tok + lax.broadcasted_iota(jnp.int32, (tok, HEAD_DIM), 0)
+    angle = spot.astype(F32) * freqs
+    cosine = jnp.cos(angle)
+    sine = jnp.sin(angle)
+    sine = jnp.where(lanes < half, -sine, sine)
+    for j in range(2):
+        cos_ref[j * tok : (j + 1) * tok] = cosine
+        sin_ref[j * tok : (j + 1) * tok] = sine
+    for c in range(nc):
+        gq_ref[c] = gq_in[c * COLS : (c + 1) * COLS].reshape(1, COLS)
+        gk_ref[c] = gk_in[c * COLS : (c + 1) * COLS].reshape(1, COLS)
     sq[...] = jnp.zeros_like(sq)
     sk[...] = jnp.zeros_like(sk)
 
     @pl.loop(0, nc)
     def _(c):
         acc = product(0, 2 * c)
+
+        @pl.when(c == 0)
+        def _():
+            pl.semaphore_wait(barrier, len(peers))
+
         sk[...] += acc[:, :HEAD_DIM] * acc[:, :HEAD_DIM] + acc[:, HEAD_DIM:] * acc[:, HEAD_DIM:]
         turned(acc, gk_ref, c, kbuf)
 
@@ -147,98 +165,77 @@
         copy.start()
         sends.append(copy)
 
-    @pl.loop(0, nc)
-    def _(c):
-        acc = product(2, 2 * nc + c).astype(BF16)
-        for j in range(2):
-            vbuf[c, j, 0:tok, :] = acc[j * tok : (j + 1) * tok]
-
-        @pl.when(z == 0)
-        def _():
-            v_copy(c, 1).start()
-
-    for c in range(max(0, RING - 1), no):
-        wo_copy(c).start()
-
-    for copy in sends:
-        copy.wait()
-
-    def total(back):
-        tot = sums_out[...] if back == 0 else None
-        n = 0
-        for dz in range(ns):
-            for dk in range(nt):
-                if dz or dk:
-                    if dz == back:
-                        tot = sums_in[n] if tot is None else tot + sums_in[n]
-                    n += 1
-        return lax.rsqrt(tot / width + 1e-06)
-
-    r0 = total(0)
-    ahead = [r0, total(ns - 1), total(ns - 2)]
-    factor = HEAD_DIM ** (-0.5)
-    for s in range(3):
-        rqs[s] = jnp.transpose(jnp.broadcast_to(ahead[s][0:1, :] * factor, (rows, rows)))
-    r1 = total(1)
-    low = lax.broadcasted_iota(jnp.int32, r0.shape, 1) < tok
-    rks[0] = jnp.where(low, r0, pltpu.roll(r1, tok, 1))
-    rks[1] = jnp.where(low, pltpu.roll(r0, tok, 1), r1)
-
-    def attend(nq, nk, has_in):
-        own_lse[...] = jnp.zeros_like(own_lse)
-        if nq > 1:
-            lse_out[...] = jnp.zeros_like(lse_out)
-        lane = lax.broadcasted_iota(jnp.int32, (tok, HEAD_DIM), 1)
+    def scales():
+        for copy in sends:
+            copy.wait()
+
+        def total(back):
+            tot = sums_out[...] if back == 0 else None
+            n = 0
+            for dz in range(ns):
+                for dk in range(nt):
+                    if dz or dk:
+                        if dz == back:
+                            tot = sums_in[n] if tot is None else tot + sums_in[n]
+                        n += 1
+            return lax.rsqrt(tot / width + 1e-06)
+
+        r0 = total(0)
+        ahead = [r0, total(ns - 1), total(ns - 2)]
+        factor = HEAD_DIM ** (-0.5)
+        for s in range(3):
+            rqs[s] = jnp.transpose(jnp.broadcast_to(ahead[s][0:1, :] * factor, (rows, rows)))
+        r1 = total(1)
+        low = lax.broadcasted_iota(jnp.int32, r0.shape, 1) < tok
+        rks[0] = jnp.where(low, r0, pltpu.roll(r1, tok, 1))
+        rks[1] = jnp.where(low, pltpu.roll(r0, tok, 1), r1)
+
+    lane = lax.broadcasted_iota(jnp.int32, (tok, HEAD_DIM), 1)
+
+    def attend(c, nq, nk, has_in):
         row = lax.broadcasted_iota(jnp.int32, (tok, nk * tok), 0)
         col = lax.broadcasted_iota(jnp.int32, (tok, nk * tok), 1)
         allowed = (col <= row) | (col >= tok)
-
-        @pl.loop(0, nc)
-        def _(c):
-            for s in range(1, nq):
-                q_copy(c, s, z).wait_recv()
-            if nk > 1:
-                k_copy(c, z).wait_recv()
-                v_copy(c, z).wait_recv()
-            for j in range(2):
-                for h in range(2):
-                    hs = slice(h * HEAD_DIM, (h + 1) * HEAD_DIM)
-                    u = c * 4 + j * 2 + h
-                    k = kbuf[c, j, 0 : nk * tok, hs]
-                    v = vbuf[c, j, 0 : nk * tok, hs]
-                    q = qbuf[c, j, 0 : nq * tok, hs]
-                    score = lax.dot_general(q, k, (((1,), (1,)), ((), ())), preferred_element_type=F32)
-                    weights, tots, tops = [], [], []
-                    for s in range(nq):
-                        sc = score[s * tok : (s + 1) * tok]
-                        sc = sc * rqs[s, j * tok : (j + 1) * tok, 0 : nk * tok] * rks[j, 1:2, 0 : nk * tok]
-                        if s == 0:
-                            sc = jnp.where(allowed, sc, -1e30)
-                        top = jnp.max(sc, axis=1, keepdims=True)
-                        e = jnp.exp(sc - top)
-                        tots.append(jnp.sum(e, axis=1, keepdims=True))
-                        tops.append(top)
-                        weights.append(e.astype(BF16))
-                    w = weights[0] if nq == 1 else jnp.concatenate(weights, axis=0)
-                    acc = jnp.dot(w, v, preferred_element_type=F32)
-                    for s in range(nq):
-                        o = acc[s * tok : (s + 1) * tok] / tots[s]
-                        if s == 0 and not has_in:
-                            mixed[j * tok : (j + 1) * tok, pl.ds(pl.multiple_of(c * COLS + h * HEAD_DIM, HEAD_DIM), HEAD_DIM)] = o.astype(BF16)
-                        elif s == 0:
-                            own_o[c, j, :, hs] = o
-                            own_lse[...] = jnp.where(lane == u, tops[s] + jnp.log(tots[s]), own_lse[...])
-                        else:
-                            oout[s - 1, c, j, :, hs] = o.astype(BF16)
-                            lse_out[s - 1] = jnp.where(lane == u, tops[s] + jnp.log(tots[s]), lse_out[s - 1])
-            for s in range(1, nq):
-                o_copy(c, s, z + s).start()
-
         for s in range(1, nq):
-            l_copy(s, z + s).start()
+            q_copy(c, s, z).wait_recv()
+        if nk > 1:
+            k_copy(c, z).wait_recv()
+            v_copy(c, z).wait_recv()
+        for j in range(2):
+            for h in range(2):
+                hs = slice(h * HEAD_DIM, (h + 1) * HEAD_DIM)
+                u = c * 4 + j * 2 + h
+                k = kbuf[c, j, 0 : nk * tok, hs]
+                v = vbuf[c, j, 0 : nk * tok, hs]
+                q = qbuf[c, j, 0 : nq * tok, hs]
+                score = lax.dot_general(q, k, (((1,), (1,)), ((), ())), preferred_element_type=F32)
+                weights, tots, tops = [], [], []
+                for s in range(nq):
+                    sc = score[s * tok : (s + 1) * tok]
+                    sc = sc * rqs[s, j * tok : (j + 1) * tok, 0 : nk * tok] * rks[j, 1:2, 0 : nk * tok]
+                    if s == 0:
+                        sc = jnp.where(allowed, sc, -1e30)
+                    top = jnp.max(sc, axis=1, keepdims=True)
+                    e = jnp.exp(sc - top)
+                    tots.append(jnp.sum(e, axis=1, keepdims=True))
+                    tops.append(top)
+                    weights.append(e.astype(BF16))
+                w = weights[0] if nq == 1 else jnp.concatenate(weights, axis=0)
+                acc = jnp.dot(w, v, preferred_element_type=F32)
+                for s in range(nq):
+                    o = acc[s * tok : (s + 1) * tok] / tots[s]
+                    if s == 0 and not has_in:
+                        mixed[j * tok : (j + 1) * tok, pl.ds(pl.multiple_of(c * COLS + h * HEAD_DIM, HEAD_DIM), HEAD_DIM)] = o.astype(BF16)
+                    elif s == 0:
+                        own_o[c, j, :, hs] = o
+                        own_lse[...] = jnp.where(lane == u, tops[s] + jnp.log(tots[s]), own_lse[...])
+                    else:
+                        oout[s - 1, c, j, :, hs] = o.astype(BF16)
+                        lse_out[s - 1] = jnp.where(lane == u, tops[s] + jnp.log(tots[s]), lse_out[s - 1])
+        for s in range(1, nq):
+            o_copy(c, s, z + s).start()
 
     def merge(ni):
-        lane = lax.broadcasted_iota(jnp.int32, (tok, HEAD_DIM), 1)
         for s in range(1, ni + 1):
             l_copy(s, z).wait_recv()
         lses = [own_lse[...]] + [lse_in[s] for s in range(ni)]
@@ -262,22 +259,51 @@
                         o += share * (own_o[c, j, :, hs] if s == 0 else oin[s - 1, c, j, :, hs].astype(F32))
                     mixed[j * tok : (j + 1) * tok, pl.ds(pl.multiple_of(c * COLS + h * HEAD_DIM, HEAD_DIM), HEAD_DIM)] = o.astype(BF16)
 
-    @pl.when(z == 0)
-    def _():
-        attend(1, 1, False)
+    own_lse[...] = jnp.zeros_like(own_lse)
+    lse_out[...] = jnp.zeros_like(lse_out)
+
+    @pl.loop(0, nc)
+    def _(c):
+        acc = product(2, 2 * nc + c).astype(BF16)
+        for j in range(2):
+            vbuf[c, j, 0:tok, :] = acc[j * tok : (j + 1) * tok]
+
+        @pl.when(z == 0)
+        def _():
+            v_copy(c, 1).start()
+
+        @pl.when(c == 0)
+        def _():
+            scales()
+
+        @pl.when(z == 0)
+        def _():
+            attend(c, 1, 1, False)
+
+        @pl.when(z == 1)
+        def _():
+            attend(c, 3, 2, False)
+
+        @pl.when(z == 2)
+        def _():
+            attend(c, 2, 1, True)
+
+        @pl.when(z == 3)
+        def _():
+            attend(c, 1, 1, True)
 
     @pl.when(z == 1)
     def _():
-        attend(3, 2, False)
+        l_copy(1, 2).start()
+        l_copy(2, 3).start()
 
     @pl.when(z == 2)
     def _():
-        attend(2, 1, True)
+        l_copy(1, 3).start()
         merge(1)
 
     @pl.when(z == 3)
     def _():
-        attend(1, 1, True)
         merge(2)
 
     share = tok // nt
@@ -351,19 +377,13 @@
     rows = tok * seqs
     width = HEADS * HEAD_DIM
     x = jnp.transpose(tokens, (1, 0, 2)).reshape(rows, depth)
-    half = HEAD_DIM // 2
-    freqs = jnp.exp(-jnp.log(500000.0) * jnp.arange(half, dtype=F32) * 2.0 / HEAD_DIM)
-    positions = lax.axis_index("seq") * tok + jnp.arange(rows, dtype=jnp.int32) % tok
-    angle = positions.astype(F32)[:, None] * freqs[None, :]
-    cosine, sine = jnp.cos(angle), jnp.sin(angle)
-    cosine = jnp.concatenate([cosine, cosine], axis=1)
-    sine = jnp.concatenate([-sine, sine], axis=1)
     peers = ns * nt - 1
     vm = pltpu.VMEM
     dma = pltpu.SemaphoreType.DMA
     tile = (tok, HEAD_DIM)
     scratch = [
         vm((RING, depth, COLS), BF16), vm((no, local, oc), BF16),
+        vm((rows, HEAD_DIM), F32), vm((rows, HEAD_DIM), F32), vm((nc, 1, COLS), F32), vm((nc, 1, COLS), F32),
         vm((rows, HEAD_DIM), F32), vm((rows, HEAD_DIM), F32),
         vm((8, rows), F32), vm((peers, 8, rows), F32),
         vm((3, rows, rows), F32), vm((2, 8, rows), F32),
@@ -382,11 +402,11 @@
     out = pl.pallas_call(
         functools.partial(block_kernel, ns, nt, tok, width),
         out_shape=jax.ShapeDtypeStruct((seqs, tok // nt, depth), BF16),
-        in_specs=[in_vmem] * 5 + [anywhere] * 4,
+        in_specs=[in_vmem] * 3 + [anywhere] * 4,
         out_specs=in_vmem,
         scratch_shapes=scratch,
         compiler_params=pltpu.CompilerParams(collective_id=0, has_side_effects=True, vmem_limit_bytes=60 * 1024 * 1024),
-    )(x, cosine, sine, gain_query.reshape(nc, 1, COLS), gain_key.reshape(nc, 1, COLS), w_query, w_key, w_value, w_out)
+    )(x, gain_query, gain_key, w_query, w_key, w_value, w_out)
     return jnp.transpose(out, (1, 0, 2))
 
 

time: 68.7 us -> 65.2 us (0.949)
  local copies, waits for them, and re-layouts: 7.27 us -> 4.67 us
  other arithmetic: 1.07 us -> 0 us
    reshape x2 -> x0, local copies, waits for them, and re-layouts: 2.6 us -> none  [the longest x1 1.3 us: fused(): gain_query.reshape(nc, 1, COLS)]
    concatenate x1 -> x0, other arithmetic: 0.75 us -> none  [fused(): cosine = jnp.concatenate([cosine, cosine], axis=1)]
where the time goes in v2:
time: 65.2 us; the launch traced here: 65 us
  Pallas kernels  60.4 us (93%)
  local copies, waits for them, and re-layouts  4.67 us (7%)
    pallas_call x1, Pallas kernels, fused(): pl.pallas_call(functools.partial(block_kernel, ns, nt, tok, width), out_s...  60.4 us
    transpose x1, local copies, waits for them, and re-layouts, fused(): x = jnp.transpose(tokens, (1, 0, 2)).reshape(rows, depth)  2.63 us
    transpose x1, local copies, waits for them, and re-layouts, fused(): return jnp.transpose(out, (1, 0, 2))  2.03 us

profile of v2, /device:TPU:24, one launch (start us, length us, event | category | flops | bytes accessed | tf_op | source)
XLA Modules:
  0.0 65.0 jit_solution(16981601227137305683)
XLA Ops:
  0.0 2.6 %copy.8 = bf16[2,64,5120]{2,1,0:T(8,128)(2,1)} copy(bf16[2,64,5120]{2,0,1:T(2,128)(2,1)} %bitcast.5) | data formatting | bytes 2621440 | tf_op jit(solution)/shard_map/transpose | solution.py:379
  2.6 60.4 %shard_map.73 = bf16[2,16,5120]{2,1,0:T(8,128)(2,1)} custom-call(bf16[128,5120]{1,0:T(8,128)(2,1)} %bitcast.3, f32[1280]{0:T(1024)} %gq_in.1, f32[1280]{0:T(1024)} %gk_in.1, bf16[5120,1280]{1,0:T(8,128)(2,1)} %wq.1, bf16[5120,1280]{1,0:T(8,128)(2,1)} %wk.1, bf16[5120,1280]{1,0:T(8,128)(2,1)} %wv.1, bf16[1280,5120]{1,0:T(8,128)(2,1)} %wo.1), custom_call_target="tpu_custom_call" | custom-call | tf_op jit(solution)/shard_map/pallas_call | solution.py:402
  63.0 2.0 %copy.9 = bf16[16,2,5120]{2,1,0:T(2,128)(2,1)} copy(bf16[16,2,5120]{2,0,1:T(8,128)(2,1)} %bitcast.4) | data formatting | bytes 655360 | tf_op jit(solution)/shard_map/transpose | solution.py:410
